TPU v7x, 256 devices: a whole 4x4x8 slice. The times are simulated.
256 devices in a mesh: shard: 32 (over z_lo, y, core), model: 8 (over z_hi, x).
Axes of the slice: x: 4, y: 4, z: 8 (z_hi: 2, z_lo: 4; z = z_hi * 4 + z_lo), core: 2. Of those that a mesh axis runs over, the one named last changes fastest.
Arguments:
- gradients: float32 [256, 128, 4096], P(None, 'shard', 'model'), may hold values from -6 to 6
- momentum: float32 [256, 128, 4096], P(None, 'shard', 'model'), may hold values from -6 to 6
- weights: float32 [256, 128, 4096], P(None, 'shard', 'model'), may hold values from -0.1875 to 0.1875
Outputs:
- new_weights: float32 [256, 128, 4096], P(None, 'shard', 'model')
- new_momentum: float32 [256, 128, 4096], P(None, 'shard', 'model')
All inputs are finite; a program needn't handle non-finite values.
Results may differ from a plain program's by a relative error of at most 0.00012.
Values sent between devices are 32-bit elements; how exact they have to be, the bound alone decides.
No kernel may reach another device: no remote copies, remote signals or barrier semaphores. Data moves between devices by JAX's collectives and lax.ppermute only.
A program may use at most 64 MiB of HBM per device.

v0:
```python
import jax
import jax.numpy as jnp
from jax import lax
from jax.sharding import Mesh
from jax.sharding import PartitionSpec as P

ITERS = 4
SHARD = ("shard_0", "shard_1", "shard_2")


hold_rate = 0.9
learn_rate = 0.8


def in_blocks(array, dim, count):
    shape = array.shape
    parts = array.reshape(*shape[:dim], count, shape[dim] // count, *shape[dim + 1 :])
    return jnp.moveaxis(parts, dim, 0)


def in_order(parts, dim):
    parts = jnp.moveaxis(parts, 0, dim)
    shape = parts.shape
    return parts.reshape(*shape[:dim], shape[dim] * shape[dim + 1], *shape[dim + 2 :])


def turned_blocks(parts, axes, turns):
    inside = parts.shape[1:]
    filled = parts.reshape(*(lax.axis_size(a) for a in axes), *inside)
    for k in turns:
        filled = lax.all_to_all(filled, axes[k], k, k, tiled=True)
    return filled.reshape(-1, *inside)


def two_step_exchange(array, groups, turns, split_dim, concat_dim):
    count = lax.axis_size(groups[0]) * lax.axis_size(groups[1])
    parts = in_blocks(array, split_dim, count)
    return in_order(turned_blocks(parts, groups, turns), concat_dim)


def local(gradients, momentum, weights):
    new_momentum = hold_rate * momentum + gradients
    direction = hold_rate * new_momentum + gradients
    moved = two_step_exchange(direction, (("shard_0", "shard_1"), "shard_2"), (1, 0), 0, 1)
    whole = lax.all_to_all(moved, "model", split_axis=0, concat_axis=2, tiled=True)
    iterate = whole * lax.rsqrt(jnp.sum(whole * whole, axis=(1, 2), keepdims=True) + 1e-06)
    for step in range(ITERS):
        gram = jnp.einsum("mik,mjk->mij", iterate, iterate, precision=lax.Precision.HIGHEST)
        mixed = -4.775 * gram + 2.0315 * jnp.einsum(
            "mij,mjk->mik", gram, gram, precision=lax.Precision.HIGHEST
        )
        iterate = 3.4445 * iterate + jnp.einsum(
            "mij,mjk->mik", mixed, iterate, precision=lax.Precision.HIGHEST
        )
    iterate = lax.all_to_all(iterate, "model", split_axis=2, concat_axis=0, tiled=True)
    back = lax.all_to_all(iterate, SHARD, split_axis=1, concat_axis=0, tiled=True)
    new_weights = weights - learn_rate * back
    return (new_weights, new_momentum)


def solution(mesh):
    finer = Mesh(
        mesh.devices.reshape(4, 4, 2, mesh.shape["model"]),
        ("shard_0", "shard_1", "shard_2", "model"),
    )
    placed = (P(None, SHARD, "model"), P(None, SHARD, "model"), P(None, SHARD, "model"))
    return jax.shard_map(
        local,
        mesh=finer,
        in_specs=placed,
        out_specs=(P(None, SHARD, "model"), P(None, SHARD, "model")),
        check_vma=False,
    )
```

profile of v0, /device:TPU:1, one launch (start us, length us, event | category | flops | bytes accessed | tf_op | source)
XLA Modules:
  0.0 271.7 jit_solution(3068615582505055109)
XLA Ops:
  0.6 4.9 %fusion.3 = (f32[256,4,512]{2,0,1:T(8,128)}, f32[256,4,512]{2,0,1:T(8,128)S(1)}) fusion(f32[256,4,512]{2,1,0:T(4,128)} %param.4, f32[256,4,512]{2,1,0:T(4,128)} %param.3), kind=kLoop, calls=%fused_computation.9 | loop fusion | flops 2097152 | bytes 8388608 | tf_op jit(solution)/shard_map/add | solution.py:42
  5.5 1.8 copy.32
  7.3 8.2 %all_to_all.46 = f32[16,2,8,4,512]{4,3,2,0,1:T(4,128)S(1)} all-to-all(f32[16,2,8,4,512]{4,3,2,0,1:T(4,128)S(1)} %copy.32), channel_id=1, replica_groups=mesh['shard_0'=4,'shard_1'=4,'shard_2'=2,'model'=8] {'shard_2'}, dimensions={1} | all-to-all | bytes 4194304 | tf_op jit(solution)/shard_map/all_to_all | solution.py:31
  15.6 0.9 copy.33
  16.4 53.8 %all_to_all.47 = f32[16,2,8,4,512]{4,2,3,1,0:T(8,128)S(1)} all-to-all(f32[16,2,8,4,512]{4,2,3,1,0:T(8,128)S(1)} %copy.33), channel_id=1, replica_groups=mesh['shard_0'=4,'shard_1'=4,'shard_2'=2,'model'=8] {'shard_0','shard_1'}, dimensions={0} | all-to-all | bytes 4194304 | tf_op jit(solution)/shard_map/all_to_all | solution.py:31
  70.2 1.2 copy.44
  71.5 35.3 %all_to_all.48 = f32[8,128,512]{2,1,0:T(8,128)S(1)} all-to-all(f32[8,128,512]{2,1,0:T(8,128)S(1)} %copy.44), channel_id=1, replica_groups=mesh['shard_0'=4,'shard_1'=4,'shard_2'=2,'model'=8] {'model'}, dimensions={0} | all-to-all | bytes 4194304 | tf_op jit(solution)/shard_map/all_to_all | solution.py:45
  106.8 1.1 multiply_reduce_fusion
  108.6 1.8 fusion.5
  110.4 0.2 fusion.11
  110.6 2.7 %multiply_bitcast_fusion.1 = (f32[1,128,8,512]{3,1,2,0:T(8,128)}, f32[1,128,8,512]{3,1,2,0:T(8,128)}) fusion(f32[8,128,512]{2,1,0:T(8,128)S(1)} %all_to_all.48, f32[]{:T(128)S(6)} %rsqrt.4), kind=kLoop, calls=%fused_computation.14 | loop fusion | flops 1048576 | bytes 6291460 | tf_op jit(solution)/shard_map/mul | solution.py:46
  113.4 1.9 copy.36
  115.3 2.9 %copy.35 = f32[1,128,8,512]{1,3,2,0:T(8,128)} copy(f32[1,128,8,512]{3,1,2,0:T(8,128)} %get-tuple-element.9) | data formatting | bytes 4194304 | tf_op jit(solution)/shard_map/mul | solution.py:52
  118.2 2.9 %copy.37 = f32[128,4096]{1,0:T(8,128)} copy(f32[128,4096]{0,1:T(8,128)} %bitcast.61) | data formatting | bytes 4194304 | tf_op jit(solution)/shard_map/mul | solution.py:52
  121.1 3.6 %convolution_add_fusion.3 = f32[128,4096]{1,0:T(8,128)S(1)} fusion(f32[128,4096]{1,0:T(8,128)} %copy.37, f32[128,128]{1,0:T(8,128)S(1)} %fusion.11, f32[128,4096]{0,1:T(8,128)S(1)} %bitcast.57), kind=kOutput, calls=%fused_computation.4 | convolution fusion | flops 805830656 | bytes 6356992 | tf_op jit(solution)/shard_map/mij,mjk->mik/dot_general | solution.py:52
  124.7 1.8 fusion.13
  126.5 0.2 fusion.10
  126.7 2.0 convolution_add_fusion.2
  128.7 1.8 fusion.14
  130.7 2.0 convolution_add_fusion.1
  132.8 1.8 fusion.15
  134.8 2.3 fusion
  137.1 3.7 %copy.38 = f32[1,128,4096]{1,0,2:T(1,128)} copy(f32[1,128,4096]{2,1,0:T(8,128)S(1)} %fusion) | data formatting | bytes 4194304 | tf_op jit(solution)/shard_map/add | solution.py:52
  140.8 23.3 %all_to_all.49 = f32[1,128,4096]{1,0,2:T(1,128)S(1)} all-to-all(f32[1,128,4096]{1,0,2:T(1,128)} %copy.38), channel_id=1, replica_groups=mesh['shard_0'=4,'shard_1'=4,'shard_2'=2,'model'=8] {'model'}, dimensions={2} | all-to-all | bytes 4194304 | tf_op jit(solution)/shard_map/all_to_all | solution.py:55
  164.1 2.0 copy.45
  166.2 52.5 %all-to-all-start.4 = ((f32[8,128,512]{2,0,1:T(8,128)}), f32[8,128,512]{2,0,1:T(8,128)S(1)}, u32[]{:S(2)}, u32[]{:S(2)}) async-start(f32[8,128,512]{2,0,1:T(8,128)} %bitcast.59), calls=%async_computation.4 | async-start | bytes 4194304 | tf_op jit(solution)/shard_map/all_to_all | solution.py:56
  218.7 4.3 %copy.43 = f32[256,4,512]{2,1,0:T(4,128)} copy(f32[256,4,512]{2,0,1:T(8,128)} %get-tuple-element.6) | data formatting | bytes 4194304
  222.9 43.7 %all-to-all-done.4 = f32[8,128,512]{2,0,1:T(8,128)S(1)} async-done(((f32[8,128,512]{2,0,1:T(8,128)}), f32[8,128,512]{2,0,1:T(8,128)S(1)}, u32[]{:S(2)}, u32[]{:S(2)}) %all-to-all-start.4) | async-done | bytes 2097184 | tf_op jit(solution)/shard_map/all_to_all | solution.py:56
  266.7 0.2 broadcast_multiply_fusion
  266.9 1.3 copy-done
  268.2 0.7 bitcast_subtract_fusion
  269.0 2.7 copy.42
  (3 shorter events, 0.4 us)
Async XLA Ops:
  166.2 100.5 %all-to-all-start.4 = ((f32[8,128,512]{2,0,1:T(8,128)}), f32[8,128,512]{2,0,1:T(8,128)S(1)}, u32[]{:S(2)}, u32[]{:S(2)}) async-start(f32[8,128,512]{2,0,1:T(8,128)} %bitcast.59), calls=%async_computation.4 | async-start | bytes 4194304 | tf_op jit(solution)/shard_map/all_to_all | solution.py:56
  266.6 1.6 copy-start
where the time goes:
time: 272 us
  blocking collectives  121 us (44%)
  starting transfers between devices  52.5 us (19%)
  waiting for transfers between devices  43.7 us (16%)
  local copies, waits for them, and re-layouts  25.6 us (9%)
  matrix products  17.9 us (7%)
  other arithmetic  9.74 us (4%)
    all_to_all x2, blocking collectives, turned_blocks(): filled = lax.all_to_all(filled, axes[k], k, k, tiled=True)  62.1 us
    all_to_all x1, starting transfers between devices, local(): lax.all_to_all(iterate, SHARD, split_axis=1, concat_axis=0, tiled=True)  52.5 us
    all_to_all x1, waiting for transfers between devices, local(): lax.all_to_all(iterate, SHARD, split_axis=1, concat_axis=0, tiled=True)  43.7 us
    all_to_all x1, blocking collectives, local(): lax.all_to_all(moved, 'model', split_axis=0, concat_axis=2, tiled=True)  35.3 us
    all_to_all x1, blocking collectives, local(): lax.all_to_all(iterate, 'model', split_axis=2, concat_axis=0, tiled=True)  23.3 us
    dot_general x4, matrix products, local(): jnp.einsum('mij,mjk->mik', mixed, iterate, precision=lax.Precision.HIGHEST)  9.94 us
    unnamed x4, local copies, waits for them, and re-layouts  8.27 us
    dot_general x4, matrix products, local(): jnp.einsum('mik,mjk->mij', iterate, iterate, precision=lax.Precision.HIGH...  7.17 us
  transfers between devices with their start and end apart: 1, of which 1 were waited for; matrix products, arithmetic and copies ran while one was open for 2% of the time, Pallas kernels for 0%

commit v1 on v0

v1 whole, which is shorter than its diff:
```python
import jax
import jax.numpy as jnp
from jax import lax
from jax.experimental import pallas as pl
from jax.experimental.pallas import tpu as pltpu
from jax.sharding import Mesh
from jax.sharding import PartitionSpec as P

ITERS = 4
SHARD = ("shard_0", "shard_1", "shard_2")
HIGH = lax.Precision.HIGHEST

hold_rate = 0.9
learn_rate = 0.8


def dot(a, b):
    return jnp.dot(a, b, precision=HIGH, preferred_element_type=jnp.float32)


def gram_body(x_ref, out_ref):
    x = x_ref[:, 0].reshape(128, x_ref.shape[-1])
    out_ref[0] = lax.dot_general(x, x, (((1,), (1,)), ((), ())), precision=HIGH, preferred_element_type=jnp.float32)


def grams(x):
    sources, mats, rows, wide = x.shape
    side = sources * rows
    return pl.pallas_call(
        gram_body,
        grid=(mats,),
        in_specs=[pl.BlockSpec((sources, 1, rows, wide), lambda i: (0, i, 0, 0))],
        out_specs=pl.BlockSpec((1, side, side), lambda i: (i, 0, 0)),
        out_shape=jax.ShapeDtypeStruct((mats, side, side), jnp.float32),
    )(x)


def chain_body(mine_ref, theirs_ref, out_ref):
    side = out_ref.shape[-1]
    row = lax.broadcasted_iota(jnp.int32, (side, side), 0)
    col = lax.broadcasted_iota(jnp.int32, (side, side), 1)
    eye = jnp.where(row == col, 1.0, 0.0)
    for i in range(out_ref.shape[0]):
        gram = mine_ref[i] + theirs_ref[i]
        scale = lax.rsqrt(jnp.sum(gram * eye, keepdims=True) + 1e-06)
        a = gram * (scale * scale)
        q = None
        for step in range(ITERS):
            p = 3.4445 * eye + (-4.775 * a + 2.0315 * dot(a, a))
            q = p * scale if q is None else dot(p, q)
            if step + 1 < ITERS:
                a = dot(p, dot(p, a))
        out_ref[i] = q


def chain(mine, theirs):
    return pl.pallas_call(
        chain_body,
        out_shape=jax.ShapeDtypeStruct(mine.shape, jnp.float32),
    )(mine, theirs)


def apply_body(q_ref, x_ref, out_ref):
    sources, _, rows, wide = x_ref.shape
    x = x_ref[:, 0].reshape(sources * rows, wide)
    out_ref[:, 0] = dot(q_ref[0], x).reshape(sources, rows, wide)


def applied(q, x):
    sources, mats, rows, wide = x.shape
    side = sources * rows
    block = pl.BlockSpec((sources, 1, rows, wide), lambda i: (0, i, 0, 0))
    return pl.pallas_call(
        apply_body,
        grid=(mats,),
        in_specs=[pl.BlockSpec((1, side, side), lambda i: (i, 0, 0)), block],
        out_specs=block,
        out_shape=jax.ShapeDtypeStruct(x.shape, jnp.float32),
    )(q, x)


def local(gradients, momentum, weights):
    new_momentum = hold_rate * momentum + gradients
    direction = hold_rate * new_momentum + gradients
    group = lax.axis_size(SHARD)
    mats, rows, wide = direction.shape
    across = lax.axis_size("x")
    x = lax.all_to_all(direction.reshape(group, mats // group, rows, wide), SHARD, 0, 0, tiled=True)
    part = grams(x)
    side = part.shape[-1]
    part = lax.all_to_all(part.reshape(across, -1, side, side), "x", 0, 0, tiled=True)
    mine = jnp.sum(part, axis=0)
    theirs = lax.ppermute(mine, "z_hi", [(0, 1), (1, 0)])
    q = chain(mine, theirs)
    q = lax.all_to_all(jnp.broadcast_to(q[None], (across, *q.shape)), "x", 0, 0, tiled=True)
    y = applied(q.reshape(-1, side, side), x)
    back = lax.all_to_all(y, SHARD, 0, 0, tiled=True).reshape(mats, rows, wide)
    return (weights - learn_rate * back, new_momentum)


def solution(mesh):
    finer = Mesh(
        mesh.devices.reshape(4, 4, 2, 2, 4),
        ("shard_0", "shard_1", "shard_2", "z_hi", "x"),
    )
    placed = P(None, SHARD, ("z_hi", "x"))
    return jax.shard_map(
        local,
        mesh=finer,
        in_specs=(placed, placed, placed),
        out_specs=(placed, placed),
        check_vma=False,
    )
```

time: 272 us -> 182 us (0.67)
  starting transfers between devices: 52.5 us -> 4.3 us
  waiting for transfers between devices: 43.7 us -> 3.57 us
  local copies, waits for them, and re-layouts: 25.6 us -> 2.57 us
  blocking collectives: 121 us -> 143 us
  Pallas kernels: 0 us -> 20.2 us
  matrix products: 17.9 us -> 0 us
    all_to_all x1 -> x0, starting transfers between devices: 52.5 us -> none  [local(): lax.all_to_all(iterate, SHARD, split_axis=1, concat_axis=0, tiled=True)]
    all_to_all x1 -> x0, waiting for transfers between devices: 43.7 us -> none  [local(): lax.all_to_all(iterate, SHARD, split_axis=1, concat_axis=0, tiled=True)]
    all_to_all x4, blocking collectives: 121 us -> 143 us  [the longest x1 60.6 us: local(): back = lax.all_to_all(y, SHARD, 0, 0, tiled=True).reshape(mats, rows, wide)]
    pallas_call x0 -> x3, Pallas kernels: none -> 20.2 us  [the longest x1 7.11 us: applied(): pl.pallas_call(apply_body, grid=(mats,), in_specs=[pl.BlockSpec((1, side,...]
    dot_general x12 -> x0, matrix products: 17.9 us -> none  [the longest x4 9.94 us: local(): jnp.einsum('mij,mjk->mik', mixed, iterate, precision=lax.Precision.HIGHEST)]
    mul x3 -> x0, local copies, waits for them, and re-layouts: 7.7 us -> none  [the longest x2 5.8 us: local(): 3.4445 * iterate]
    unnamed x4 -> x6, local copies, waits for them, and re-layouts: 8.27 us -> 1.63 us
    ppermute x0 -> x1, starting transfers between devices: none -> 4.3 us  [local(): theirs = lax.ppermute(mine, 'z_hi', [(0, 1), (1, 0)])]
  transfers between devices with their start and end apart: 1 -> 1, of which waited for: 1 -> 1; matrix products, arithmetic and copies ran while one was open for 2% -> 0% of each run, Pallas kernels for 0% -> 0%
where the time goes in v1:
time: 182 us
  blocking collectives  143 us (79%)
  Pallas kernels  20.2 us (11%)
  other arithmetic  7.27 us (4%)
  starting transfers between devices  4.3 us (2%)
  waiting for transfers between devices  3.57 us (2%)
  local copies, waits for them, and re-layouts  2.57 us (1%)
    all_to_all x1, blocking collectives, local(): back = lax.all_to_all(y, SHARD, 0, 0, tiled=True).reshape(mats, rows, wide)  60.6 us
    all_to_all x1, blocking collectives, local(): lax.all_to_all(direction.reshape(group, mats // group, rows, wide), SHARD...  59.2 us
    all_to_all x1, blocking collectives, local(): lax.all_to_all(part.reshape(across, -1, side, side), 'x', 0, 0, tiled=True)  13.2 us
    all_to_all x1, blocking collectives, local(): lax.all_to_all(jnp.broadcast_to(q[None], (across, *q.shape)), 'x', 0, 0,...  10 us
    pallas_call x1, Pallas kernels, applied(): pl.pallas_call(apply_body, grid=(mats,), in_specs=[pl.BlockSpec((1, side,...  7.11 us
    pallas_call x1, Pallas kernels, grams(): pl.pallas_call(gram_body, grid=(mats,), in_specs=[pl.BlockSpec((sources,...  6.75 us
    pallas_call x1, Pallas kernels, chain(): pl.pallas_call(chain_body, out_shape=jax.ShapeDtypeStruct(mine.shape, jnp...  6.34 us
    add x1, other arithmetic, local(): direction = hold_rate * new_momentum + gradients  4.62 us
  transfers between devices with their start and end apart: 1, of which 1 were waited for; matrix products, arithmetic and copies ran while one was open for 0% of the time, Pallas kernels for 0%

profile of v1, /device:TPU:1, one launch (start us, length us, event | category | flops | bytes accessed | tf_op | source)
XLA Modules:
  0.0 181.6 jit_solution(9588241301616745289)
XLA Ops:
  0.6 4.6 %multiply_add_fusion = (f32[256,4,512]{2,1,0:T(4,128)S(1)}, f32[256,4,512]{2,1,0:T(4,128)}) fusion(f32[256,4,512]{2,1,0:T(4,128)} %param.3, f32[256,4,512]{2,1,0:T(4,128)} %param.4), kind=kLoop, calls=%fused_computation.1 | loop fusion | flops 2097152 | bytes 8388608 | tf_op jit(solution)/shard_map/add | solution.py:84
  5.2 59.2 %all_to_all.20.x_ref = f32[32,8,4,512]{3,2,1,0:T(4,128)} all-to-all(f32[32,8,4,512]{3,2,1,0:T(4,128)S(1)} %bitcast.5), channel_id=1, replica_groups=mesh['shard_0'=4,'shard_1'=4,'shard_2'=2,'z_hi'=2,'x'=4] {'shard_0','sha..., dimensions={0} | all-to-all | bytes 4194304 | tf_op jit(solution)/shard_map/all_to_all | solution.py:88
  64.4 6.7 %shard_map.50 = f32[8,128,128]{2,1,0:T(8,128)} custom-call(f32[32,8,4,512]{3,2,1,0:T(4,128)} %all_to_all.20.x_ref), custom_call_target="tpu_custom_call" | custom-call | tf_op jit(solution)/shard_map/pallas_call | solution.py:29
  71.2 13.2 %all_to_all.21 = f32[4,2,128,128]{3,2,1,0:T(8,128)S(1)} all-to-all(f32[4,2,128,128]{3,2,1,0:T(8,128)} %bitcast.7), channel_id=1, replica_groups=mesh['shard_0'=4,'shard_1'=4,'shard_2'=2,'z_hi'=2,'x'=4] {'x'}, dimensions={0} | all-to-all | bytes 1048576 | tf_op jit(solution)/shard_map/all_to_all | solution.py:91
  84.4 0.0 copy-start.1
  84.4 4.3 %collective-permute-start = (f32[2,128,128]{2,1,0:T(8,128)S(1)}, f32[2,128,128]{2,1,0:T(8,128)S(1)}, u32[]{:S(2)}, u32[]{:S(2)}) collective-permute-start(f32[2,128,128]{2,1,0:T(8,128)S(1)} %reduce_sum.9.mine_ref), channel_id=1, source_target_pairs={{0,4},{4,0},{1,5},{5,1},{2,6},{6,2},{3,7},{7,3},{8,12},{12,8},{9,1... | collective-permute-start | bytes 393224 | tf_op jit(solution)/shard_map/ppermute | solution.py:93
  88.7 3.6 %collective-permute-done.theirs_ref = f32[2,128,128]{2,1,0:T(8,128)S(1)} collective-permute-done((f32[2,128,128]{2,1,0:T(8,128)S(1)}, f32[2,128,128]{2,1,0:T(8,128)S(1)}, u32[]{:S(2)}, u32[]{:S(2)}) %collective-permute-start) | collective-permute-done | bytes 131104 | tf_op jit(solution)/shard_map/ppermute | solution.py:93
  92.3 0.0 copy-done.1
  92.3 0.0 copy-start.2
  92.3 0.7 copy-done.2
  93.0 6.3 %shard_map.51 = f32[2,128,128]{2,1,0:T(8,128)} custom-call(f32[2,128,128]{2,1,0:T(8,128)} %copy-done.1, f32[2,128,128]{2,1,0:T(8,128)} %copy-done.2), custom_call_target="tpu_custom_call" | custom-call | tf_op jit(solution)/shard_map/pallas_call | solution.py:57
  99.3 0.9 broadcast_in_dim.2
  100.3 10.0 %all_to_all.22 = f32[4,2,128,128]{3,2,1,0:T(8,128)} all-to-all(f32[4,2,128,128]{3,2,1,0:T(8,128)S(1)} %broadcast_in_dim.2), channel_id=1, replica_groups=mesh['shard_0'=4,'shard_1'=4,'shard_2'=2,'z_hi'=2,'x'=4] {'x'}, dimensions={0} | all-to-all | bytes 1048576 | tf_op jit(solution)/shard_map/all_to_all | solution.py:95
  110.3 7.1 %shard_map.52 = f32[32,8,4,512]{3,2,1,0:T(4,128)} custom-call(f32[8,128,128]{2,1,0:T(8,128)} %bitcast.6, f32[32,8,4,512]{3,2,1,0:T(4,128)} %all_to_all.20.x_ref), custom_call_target="tpu_custom_call" | custom-call | tf_op jit(solution)/shard_map/pallas_call | solution.py:73
  117.4 60.6 %all_to_all.23 = f32[32,8,4,512]{3,2,1,0:T(4,128)S(1)} all-to-all(f32[32,8,4,512]{3,2,1,0:T(4,128)} %shard_map.52), channel_id=1, replica_groups=mesh['shard_0'=4,'shard_1'=4,'shard_2'=2,'z_hi'=2,'x'=4] {'shard_0','sha..., dimensions={0} | all-to-all | bytes 4194304 | tf_op jit(solution)/shard_map/all_to_all | solution.py:97
  178.0 0.0 copy-start
  178.0 0.6 broadcast_multiply_fusion
  178.7 1.0 copy-done
  179.6 2.0 %bitcast_subtract_fusion = f32[256,4,512]{2,1,0:T(4,128)} fusion(f32[256,4,512]{2,1,0:T(4,128)S(1)} %copy-done, f32[32,8,4,512]{3,2,1,0:T(4,128)S(1)} %broadcast_multiply_fusion), kind=kLoop, calls=%fused_computation | loop fusion | flops 524288 | bytes 6291456 | tf_op jit(solution)/shard_map/sub | solution.py:98
  (1 shorter events, 0.0 us)
Async XLA Ops:
  84.4 7.9 %copy-start.1 = (f32[2,128,128]{2,1,0:T(8,128)}, f32[2,128,128]{2,1,0:T(8,128)S(1)}, u32[]{:S(2)}) copy-start(f32[2,128,128]{2,1,0:T(8,128)S(1)} %reduce_sum.9.mine_ref) | copy-start | bytes 393220
  84.4 7.9 %collective-permute-start = (f32[2,128,128]{2,1,0:T(8,128)S(1)}, f32[2,128,128]{2,1,0:T(8,128)S(1)}, u32[]{:S(2)}, u32[]{:S(2)}) collective-permute-start(f32[2,128,128]{2,1,0:T(8,128)S(1)} %reduce_sum.9.mine_ref), channel_id=1, source_target_pairs={{0,4},{4,0},{1,5},{5,1},{2,6},{6,2},{3,7},{7,3},{8,12},{12,8},{9,1... | collective-permute-start | bytes 393224 | tf_op jit(solution)/shard_map/ppermute | solution.py:93
  92.3 0.7 copy-start.2
  178.0 1.6 copy-start

commit v2 on v0

v2 whole, which is shorter than its diff:
```python
import jax
import jax.numpy as jnp
from jax import lax
from jax.experimental import pallas as pl
from jax.experimental.pallas import tpu as pltpu
from jax.sharding import Mesh
from jax.sharding import PartitionSpec as P

ITERS = 4
SHARD = ("shard_0", "shard_1", "shard_2")
HIGH = lax.Precision.HIGHEST

hold_rate = 0.9
learn_rate = 0.8


def dot(a, b):
    return jnp.dot(a, b, precision=HIGH, preferred_element_type=jnp.float32)


def polynomial(gram):
    side = gram.shape[-1]
    row = lax.broadcasted_iota(jnp.int32, (side, side), 0)
    col = lax.broadcasted_iota(jnp.int32, (side, side), 1)
    eye = jnp.where(row == col, 1.0, 0.0)
    scale = lax.rsqrt(jnp.sum(gram * eye, keepdims=True) + 1e-06)
    a = gram * (scale * scale)
    q = None
    for step in range(ITERS):
        p = 3.4445 * eye + (-4.775 * a + 2.0315 * dot(a, a))
        q = p * scale if q is None else dot(p, q)
        if step + 1 < ITERS:
            a = dot(p, dot(p, a))
    return q


def update_body(x_ref, out_ref):
    sources, parts, rows, wide = x_ref.shape
    side = sources * rows
    gram = None
    for part in range(parts):
        x = x_ref[:, part].reshape(side, wide)
        product = lax.dot_general(x, x, (((1,), (1,)), ((), ())), precision=HIGH, preferred_element_type=jnp.float32)
        gram = product if gram is None else gram + product
    q = polynomial(gram)
    for part in range(parts):
        x = x_ref[:, part].reshape(side, wide)
        out_ref[:, part] = dot(q, x).reshape(sources, rows, wide)


def updated(x):
    return pl.pallas_call(
        update_body,
        in_specs=[pl.BlockSpec(memory_space=pltpu.VMEM)],
        out_specs=pl.BlockSpec(memory_space=pltpu.VMEM),
        out_shape=jax.ShapeDtypeStruct(x.shape, jnp.float32),
    )(x)


def local(gradients, momentum, weights):
    new_momentum = hold_rate * momentum + gradients
    direction = hold_rate * new_momentum + gradients
    mats, rows, wide = direction.shape
    sources = lax.axis_size(SHARD)
    every = (*SHARD, "model")
    x = lax.all_to_all(direction, every, 0, 0, tiled=True)
    y = updated(x.reshape(sources, -1, rows, wide))
    back = lax.all_to_all(y.reshape(mats, rows, wide), every, 0, 0, tiled=True)
    return (weights - learn_rate * back, new_momentum)


def solution(mesh):
    finer = Mesh(
        mesh.devices.reshape(4, 4, 2, mesh.shape["model"]),
        (*SHARD, "model"),
    )
    placed = P(None, SHARD, "model")
    return jax.shard_map(
        local,
        mesh=finer,
        in_specs=(placed, placed, placed),
        out_specs=(placed, placed),
        check_vma=False,
    )
```

time: 272 us -> 149 us (0.55)
  starting transfers between devices: 52.5 us -> 0 us
  waiting for transfers between devices: 43.7 us -> 0 us
  local copies, waits for them, and re-layouts: 25.6 us -> 0.01 us
  matrix products: 17.9 us -> 0 us
  Pallas kernels: 0 us -> 11.7 us
  blocking collectives: 121 us -> 130 us
  other arithmetic: 9.74 us -> 6.66 us
    all_to_all x1 -> x0, starting transfers between devices: 52.5 us -> none  [local(): lax.all_to_all(iterate, SHARD, split_axis=1, concat_axis=0, tiled=True)]
    all_to_all x1 -> x0, waiting for transfers between devices: 43.7 us -> none  [local(): lax.all_to_all(iterate, SHARD, split_axis=1, concat_axis=0, tiled=True)]
    dot_general x12 -> x0, matrix products: 17.9 us -> none  [the longest x4 9.94 us: local(): jnp.einsum('mij,mjk->mik', mixed, iterate, precision=lax.Precision.HIGHEST)]
    pallas_call x0 -> x1, Pallas kernels: none -> 11.7 us  [updated(): pl.pallas_call(update_body, in_specs=[pl.BlockSpec(memory_space=pltpu.VME...]
    all_to_all x4 -> x2, blocking collectives: 121 us -> 130 us  [the longest x1 69.4 us: local(): x = lax.all_to_all(direction, every, 0, 0, tiled=True)]
    unnamed x4 -> x2, local copies, waits for them, and re-layouts: 8.27 us -> 0.01 us
    mul x3 -> x0, local copies, waits for them, and re-layouts: 7.7 us -> none  [the longest x2 5.8 us: local(): 3.4445 * iterate]
    add x1 -> x0, local copies, waits for them, and re-layouts: 3.7 us -> none  [local(): 3.4445 * iterate]
  transfers between devices with their start and end apart: 1 -> 0, of which waited for: 1 -> 0; matrix products, arithmetic and copies ran while one was open for 2% -> 0% of each run, Pallas kernels for 0% -> 0%
where the time goes in v2:
time: 149 us
  blocking collectives  130 us (87%)
  Pallas kernels  11.7 us (8%)
  other arithmetic  6.66 us (4%)
    all_to_all x1, blocking collectives, local(): x = lax.all_to_all(direction, every, 0, 0, tiled=True)  69.4 us
    all_to_all x1, blocking collectives, local(): back = lax.all_to_all(y.reshape(mats, rows, wide), every, 0, 0, tiled=True)  60.4 us
    pallas_call x1, Pallas kernels, updated(): pl.pallas_call(update_body, in_specs=[pl.BlockSpec(memory_space=pltpu.VME...  11.7 us
    add x1, other arithmetic, local(): direction = hold_rate * new_momentum + gradients  4.62 us

profile of v2, /device:TPU:1, one launch (start us, length us, event | category | flops | bytes accessed | tf_op | source)
XLA Modules:
  0.0 148.8 jit_solution(5383635892259471755)
XLA Ops:
  0.6 4.6 %multiply_add_fusion = (f32[256,4,512]{2,1,0:T(4,128)S(1)}, f32[256,4,512]{2,1,0:T(4,128)}) fusion(f32[256,4,512]{2,1,0:T(4,128)} %param.3, f32[256,4,512]{2,1,0:T(4,128)} %param.4), kind=kLoop, calls=%fused_computation.1 | loop fusion | flops 2097152 | bytes 8388608 | tf_op jit(solution)/shard_map/add | solution.py:62
  5.2 69.4 %all_to_all.10 = f32[256,4,512]{2,1,0:T(4,128)} all-to-all(f32[256,4,512]{2,1,0:T(4,128)S(1)} %get-tuple-element.2), channel_id=1, replica_groups=mesh['shard_0'=4,'shard_1'=4,'shard_2'=2,'model'=8] {'shard_0','shard_1'..., dimensions={0} | all-to-all | bytes 4194304 | tf_op jit(solution)/shard_map/all_to_all | solution.py:66
  74.7 11.7 %shard_map.50 = f32[32,8,4,512]{3,2,1,0:T(4,128)} custom-call(f32[32,8,4,512]{3,2,1,0:T(4,128)} %bitcast.2), custom_call_target="tpu_custom_call" | custom-call | tf_op jit(solution)/shard_map/pallas_call | solution.py:52
  86.4 0.0 copy-start
  86.4 60.4 %all_to_all.11 = f32[256,4,512]{2,1,0:T(4,128)S(1)} all-to-all(f32[256,4,512]{2,1,0:T(4,128)} %bitcast.3), channel_id=1, replica_groups=mesh['shard_0'=4,'shard_1'=4,'shard_2'=2,'model'=8] {'shard_0','shard_1'..., dimensions={0} | all-to-all | bytes 4194304 | tf_op jit(solution)/shard_map/all_to_all | solution.py:68
  146.8 0.0 copy-done
  146.8 2.0 %multiply_subtract_fusion = f32[256,4,512]{2,1,0:T(4,128)} fusion(f32[256,4,512]{2,1,0:T(4,128)S(1)} %copy-done, f32[256,4,512]{2,1,0:T(4,128)S(1)} %all_to_all.11), kind=kLoop, calls=%fused_computation | loop fusion | flops 1048576 | bytes 6291456 | tf_op jit(solution)/shard_map/sub | solution.py:69
Async XLA Ops:
  86.4 60.4 %copy-start = (f32[256,4,512]{2,1,0:T(4,128)S(1)}, f32[256,4,512]{2,1,0:T(4,128)}, u32[]{:S(2)}) copy-start(f32[256,4,512]{2,1,0:T(4,128)} %param.5) | copy-start | bytes 6291460

commit v3 on v2

v3 whole, which is shorter than its diff:
```python
import jax
import jax.numpy as jnp
from jax import lax
from jax.experimental import pallas as pl
from jax.experimental.pallas import tpu as pltpu
from jax.sharding import Mesh
from jax.sharding import PartitionSpec as P

ITERS = 4
SHARD = ("shard_0", "shard_1", "shard_2")

hold_rate = 0.9
learn_rate = 0.8


STEPS = 8


def direction_body(gradients_ref, momentum_ref, out_ref, new_ref, first_ref, second_ref, arrived):
    step = out_ref.shape[0] // STEPS

    def copies(i):
        rows = pl.ds(i * step, step)
        return (
            pltpu.make_async_copy(gradients_ref.at[rows], first_ref.at[rows], arrived.at[0, i]),
            pltpu.make_async_copy(momentum_ref.at[rows], second_ref.at[rows], arrived.at[1, i]),
        )

    for i in range(STEPS):
        for copy in copies(i):
            copy.start()
    for i in range(STEPS):
        for copy in copies(i):
            copy.wait()
        rows = pl.ds(i * step, step)
        gradients = first_ref[rows]
        new_momentum = hold_rate * second_ref[rows] + gradients
        new_ref[rows] = new_momentum
        out_ref[rows] = hold_rate * new_momentum + gradients


def direction_of(gradients, momentum):
    whole = pltpu.VMEM(gradients.shape, gradients.dtype)
    return pl.pallas_call(
        direction_body,
        in_specs=[pl.BlockSpec(memory_space=pltpu.HBM), pl.BlockSpec(memory_space=pltpu.HBM)],
        out_specs=[pl.BlockSpec(memory_space=pltpu.VMEM), pl.BlockSpec(memory_space=pltpu.VMEM)],
        out_shape=[whole, whole],
        scratch_shapes=[whole, whole, pltpu.SemaphoreType.DMA((2, STEPS))],
        compiler_params=pltpu.CompilerParams(vmem_limit_bytes=16 << 20),
    )(pltpu.with_memory_space_constraint(gradients, pltpu.HBM), pltpu.with_memory_space_constraint(momentum, pltpu.HBM))


def in_parts(x):
    first = x.astype(jnp.bfloat16)
    rest = x - first.astype(jnp.float32)
    second = rest.astype(jnp.bfloat16)
    third = (rest - second.astype(jnp.float32)).astype(jnp.bfloat16)
    return first, second, third


def on_left(a):
    first, second, third = in_parts(a)
    return jnp.concatenate([first, first, second, second, first, third], axis=1)


def on_right(b):
    first, second, third = in_parts(b)
    return jnp.concatenate([first, second, first, second, third, first], axis=0)


def product(left, right):
    return jnp.dot(left, right, preferred_element_type=jnp.float32)


def polynomial(gram):
    side = gram.shape[-1]
    row = lax.broadcasted_iota(jnp.int32, (side, side), 0)
    col = lax.broadcasted_iota(jnp.int32, (side, side), 1)
    eye = jnp.where(row == col, 1.0, 0.0)
    scale = lax.rsqrt(jnp.sum(gram * eye, keepdims=True) + 1e-06)
    a = gram * (scale * scale)
    q = eye * scale
    for step in range(ITERS):
        square = product(on_left(a), on_right(a))
        p = 3.4445 * eye + (-4.775 * a + 2.0315 * square)
        if step + 1 == ITERS:
            return product(on_left(p), on_right(q))
        left = on_left(p)
        if step == 0:
            q = p * scale
            once = product(left, on_right(a))
        else:
            both = product(left, on_right(jnp.concatenate([a, q], axis=1)))
            once, q = both[:, :side], both[:, side:]
        a = product(left, on_right(once))


def update_body(x_ref, momentum_ref, out_ref, kept_ref, written):
    keep = pltpu.make_async_copy(momentum_ref, kept_ref, written)
    keep.start()
    sources, parts, rows, wide = x_ref.shape
    side = sources * rows
    sums = None
    for part in range(parts):
        x = x_ref[:, part].reshape(side, wide)
        pieces = jnp.concatenate(in_parts(x), axis=0)
        new = lax.dot_general(
            pieces, pieces[: 2 * side], (((1,), (1,)), ((), ())), preferred_element_type=jnp.float32
        )
        sums = new if sums is None else sums + new
    small = sums[2 * side :, :side]
    small = (small + small.T) + sums[side : 2 * side, side:]
    small = small + (sums[side : 2 * side, :side] + sums[:side, side:])
    q = on_left(polynomial(sums[:side, :side] + small))
    for part in range(parts):
        x = x_ref[:, part].reshape(side, wide)
        out_ref[:, part] = product(q, on_right(x)).reshape(sources, rows, wide)
    keep.wait()


def updated(x, momentum):
    return pl.pallas_call(
        update_body,
        in_specs=[pl.BlockSpec(memory_space=pltpu.VMEM), pl.BlockSpec(memory_space=pltpu.VMEM)],
        out_specs=[pl.BlockSpec(memory_space=pltpu.VMEM), pl.BlockSpec(memory_space=pltpu.HBM)],
        out_shape=[pltpu.VMEM(x.shape, x.dtype), pltpu.HBM(momentum.shape, momentum.dtype)],
        scratch_shapes=[pltpu.SemaphoreType.DMA],
        compiler_params=pltpu.CompilerParams(vmem_limit_bytes=16 << 20),
    )(pltpu.with_memory_space_constraint(x, pltpu.VMEM), pltpu.with_memory_space_constraint(momentum, pltpu.VMEM))


def local(gradients, momentum, weights):
    direction, new_momentum = direction_of(gradients, momentum)
    mats, rows, wide = direction.shape
    sources = lax.axis_size(SHARD)
    every = (*SHARD, "model")
    x = lax.all_to_all(direction, every, 0, 0, tiled=True)
    y, new_momentum = updated(x.reshape(sources, -1, rows, wide), new_momentum)
    back = lax.all_to_all(y.reshape(mats, rows, wide), every, 0, 0, tiled=True)
    return (weights - learn_rate * back, new_momentum)


def solution(mesh):
    finer = Mesh(
        mesh.devices.reshape(4, 4, 2, mesh.shape["model"]),
        (*SHARD, "model"),
    )
    placed = P(None, SHARD, "model")
    return jax.shard_map(
        local,
        mesh=finer,
        in_specs=(placed, placed, placed),
        out_specs=(placed, placed),
        check_vma=False,
    )
```

time: 149 us -> 140 us (0.940)
  other arithmetic: 6.66 us -> 2.04 us
  Pallas kernels: 11.7 us -> 8.01 us
    pallas_call x1, Pallas kernels: 11.7 us -> 5.67 us  [updated(): pl.pallas_call(update_body, in_specs=[pl.BlockSpec(memory_space=pltpu.VME...]
    add x1 -> x0, other arithmetic: 4.62 us -> none  [local(): direction = hold_rate * new_momentum + gradients]
    pallas_call x0 -> x1, Pallas kernels: none -> 2.34 us  [direction_of(): pl.pallas_call(direction_body, in_specs=[pl.BlockSpec(memory_space=pltpu....]
where the time goes in v3:
time: 140 us
  blocking collectives  129 us (92%)
  Pallas kernels  8.01 us (6%)
  other arithmetic  2.04 us (1%)
    all_to_all x1, blocking collectives, local(): x = lax.all_to_all(direction, every, 0, 0, tiled=True)  69.3 us
    all_to_all x1, blocking collectives, local(): back = lax.all_to_all(y.reshape(mats, rows, wide), every, 0, 0, tiled=True)  59.7 us
    pallas_call x1, Pallas kernels, updated(): pl.pallas_call(update_body, in_specs=[pl.BlockSpec(memory_space=pltpu.VME...  5.67 us

profile of v3, /device:TPU:1, one launch (start us, length us, event | category | flops | bytes accessed | tf_op | source)
XLA Modules:
  0.0 139.8 jit_solution(16873389853741608189)
XLA Ops:
  0.6 2.3 %shard_map.50 = (f32[256,4,512]{2,1,0:T(4,128)S(1)}, f32[256,4,512]{2,1,0:T(4,128)S(1)}) custom-call(f32[256,4,512]{2,1,0:T(4,128)} %gradients_ref.1, f32[256,4,512]{2,1,0:T(4,128)} %momentum_ref.1), custom_call_target="tpu_custom_call" | custom-call | tf_op jit(solution)/shard_map/pallas_call | solution.py:44
  3.0 69.3 %all_to_all.10 = f32[256,4,512]{2,1,0:T(4,128)S(1)} all-to-all(f32[256,4,512]{2,1,0:T(4,128)S(1)} %get-tuple-element.6), channel_id=1, replica_groups=mesh['shard_0'=4,'shard_1'=4,'shard_2'=2,'model'=8] {'shard_0','shard_1'..., dimensions={0} | all-to-all | bytes 4194304 | tf_op jit(solution)/shard_map/all_to_all | solution.py:138
  72.3 5.7 %shard_map.51 = (f32[32,8,4,512]{3,2,1,0:T(4,128)S(1)}, f32[256,4,512]{2,1,0:T(4,128)}) custom-call(f32[32,8,4,512]{3,2,1,0:T(4,128)S(1)} %bitcast.2, f32[256,4,512]{2,1,0:T(4,128)S(1)} %get-tuple-element.7.momentum_ref), custom_call_target="tpu_custom_call" | custom-call | tf_op jit(solution)/shard_map/pallas_call | solution.py:123
  78.0 0.0 copy-start
  78.0 59.7 %all_to_all.11 = f32[256,4,512]{2,1,0:T(4,128)S(1)} all-to-all(f32[256,4,512]{2,1,0:T(4,128)S(1)} %bitcast.3), channel_id=1, replica_groups=mesh['shard_0'=4,'shard_1'=4,'shard_2'=2,'model'=8] {'shard_0','shard_1'..., dimensions={0} | all-to-all | bytes 4194304 | tf_op jit(solution)/shard_map/all_to_all | solution.py:140
  137.7 0.0 copy-done
  137.7 2.0 %multiply_subtract_fusion = f32[256,4,512]{2,1,0:T(4,128)} fusion(f32[256,4,512]{2,1,0:T(4,128)S(1)} %copy-done, f32[256,4,512]{2,1,0:T(4,128)S(1)} %all_to_all.11), kind=kLoop, calls=%fused_computation | loop fusion | flops 1048576 | bytes 6291456 | tf_op jit(solution)/shard_map/sub | solution.py:141
Async XLA Ops:
  78.0 59.7 %copy-start = (f32[256,4,512]{2,1,0:T(4,128)S(1)}, f32[256,4,512]{2,1,0:T(4,128)}, u32[]{:S(2)}) copy-start(f32[256,4,512]{2,1,0:T(4,128)} %param.5) | copy-start | bytes 6291460

commit v4 on v3

--- a/solution.py
+++ b/solution.py
@@ -8,12 +8,14 @@
 
 ITERS = 4
 SHARD = ("shard_0", "shard_1", "shard_2")
+MODEL = ("model_0", "model_1")
+EVERY = ("shard_2", "model_0", "shard_0", "shard_1", "model_1")
+STEPS = 8
 
 hold_rate = 0.9
 learn_rate = 0.8
 
-
-STEPS = 8
+limits = pltpu.CompilerParams(vmem_limit_bytes=16 << 20)
 
 
 def direction_body(gradients_ref, momentum_ref, out_ref, new_ref, first_ref, second_ref, arrived):
@@ -47,8 +49,11 @@
         out_specs=[pl.BlockSpec(memory_space=pltpu.VMEM), pl.BlockSpec(memory_space=pltpu.VMEM)],
         out_shape=[whole, whole],
         scratch_shapes=[whole, whole, pltpu.SemaphoreType.DMA((2, STEPS))],
-        compiler_params=pltpu.CompilerParams(vmem_limit_bytes=16 << 20),
-    )(pltpu.with_memory_space_constraint(gradients, pltpu.HBM), pltpu.with_memory_space_constraint(momentum, pltpu.HBM))
+        compiler_params=limits,
+    )(
+        pltpu.with_memory_space_constraint(gradients, pltpu.HBM),
+        pltpu.with_memory_space_constraint(momentum, pltpu.HBM),
+    )
 
 
 def in_parts(x):
@@ -70,7 +75,10 @@
 
 
 def product(left, right):
-    return jnp.dot(left, right, preferred_element_type=jnp.float32)
+    half = left.shape[0] // 2
+    upper = jnp.dot(left[:half], right, preferred_element_type=jnp.float32)
+    lower = jnp.dot(left[half:], right, preferred_element_type=jnp.float32)
+    return jnp.concatenate([upper, lower], axis=0)
 
 
 def polynomial(gram):
@@ -84,9 +92,9 @@
     for step in range(ITERS):
         square = product(on_left(a), on_right(a))
         p = 3.4445 * eye + (-4.775 * a + 2.0315 * square)
+        left = on_left(p)
         if step + 1 == ITERS:
-            return product(on_left(p), on_right(q))
-        left = on_left(p)
+            return product(left, on_right(q))
         if step == 0:
             q = p * scale
             once = product(left, on_right(a))
@@ -96,57 +104,90 @@
         a = product(left, on_right(once))
 
 
-def update_body(x_ref, momentum_ref, out_ref, kept_ref, written):
+def update_body(x_ref, momentum_ref, out_ref, kept_ref, pieces_ref, written):
     keep = pltpu.make_async_copy(momentum_ref, kept_ref, written)
     keep.start()
-    sources, parts, rows, wide = x_ref.shape
-    side = sources * rows
-    sums = None
-    for part in range(parts):
-        x = x_ref[:, part].reshape(side, wide)
-        pieces = jnp.concatenate(in_parts(x), axis=0)
-        new = lax.dot_general(
-            pieces, pieces[: 2 * side], (((1,), (1,)), ((), ())), preferred_element_type=jnp.float32
-        )
-        sums = new if sums is None else sums + new
-    small = sums[2 * side :, :side]
-    small = (small + small.T) + sums[side : 2 * side, side:]
-    small = small + (sums[side : 2 * side, :side] + sums[:side, side:])
-    q = on_left(polynomial(sums[:side, :side] + small))
-    for part in range(parts):
-        x = x_ref[:, part].reshape(side, wide)
-        out_ref[:, part] = product(q, on_right(x)).reshape(sources, rows, wide)
+    side = pieces_ref.shape[0] // 3
+    wide = x_ref.shape[-1]
+    parts = [(i, j) for i in range(x_ref.shape[1]) for j in range(x_ref.shape[4])]
+    upper = lower = None
+    for k, (i, j) in enumerate(parts):
+        first, second, third = in_parts(x_ref[:, i, :, :, j].reshape(side, wide))
+        pieces = jnp.concatenate([third, first, second], axis=0)
+        pieces_ref[:, k * wide : (k + 1) * wide] = pieces
+        half = pieces.shape[0] // 2
+        sums = [
+            lax.dot_general(rows, pieces[side:], (((1,), (1,)), ((), ())), preferred_element_type=jnp.float32)
+            for rows in (pieces[:half], pieces[half:])
+        ]
+        upper = sums[0] if upper is None else upper + sums[0]
+        lower = sums[1] if lower is None else lower + sums[1]
+    sums = jnp.concatenate([upper, lower], axis=0)
+    small = sums[:side, :side]
+    small = (small + small.T) + sums[2 * side :, side:]
+    small = small + (sums[2 * side :, :side] + sums[side : 2 * side, side:])
+    left = on_left(polynomial(sums[side : 2 * side, :side] + small))
+    for k, (i, j) in enumerate(parts):
+        columns = slice(k * wide, (k + 1) * wide)
+        large = pieces_ref[side:, columns]
+        right = jnp.concatenate([large, large, pieces_ref[: 2 * side, columns]], axis=0)
+        new = jnp.dot(left, right, preferred_element_type=jnp.float32)
+        out_ref[:, i, :, :, j] = new.reshape(out_ref[:, i, :, :, j].shape)
     keep.wait()
 
 
 def updated(x, momentum):
+    _, halves, _, _, blocks, _, wide = x.shape
+    columns = halves * blocks * wide
     return pl.pallas_call(
         update_body,
         in_specs=[pl.BlockSpec(memory_space=pltpu.VMEM), pl.BlockSpec(memory_space=pltpu.VMEM)],
         out_specs=[pl.BlockSpec(memory_space=pltpu.VMEM), pl.BlockSpec(memory_space=pltpu.HBM)],
         out_shape=[pltpu.VMEM(x.shape, x.dtype), pltpu.HBM(momentum.shape, momentum.dtype)],
-        scratch_shapes=[pltpu.SemaphoreType.DMA],
-        compiler_params=pltpu.CompilerParams(vmem_limit_bytes=16 << 20),
+        scratch_shapes=[
+            pltpu.VMEM((3 * x.size // columns, columns), jnp.bfloat16),
+            pltpu.SemaphoreType.DMA,
+        ],
+        compiler_params=limits,
     )(pltpu.with_memory_space_constraint(x, pltpu.VMEM), pltpu.with_memory_space_constraint(momentum, pltpu.VMEM))
+
+
+def finish_body(weights_ref, back_ref, out_ref, new_ref, written):
+    step = out_ref.shape[0] // STEPS
+    copies = []
+    for i in range(STEPS):
+        rows = pl.ds(i * step, step)
+        new_ref[rows] = weights_ref[rows] - learn_rate * back_ref[rows]
+        copies.append(pltpu.make_async_copy(new_ref.at[rows], out_ref.at[rows], written.at[i]))
+        copies[-1].start()
+    for copy in copies:
+        copy.wait()
+
+
+def finished(weights, back):
+    return pl.pallas_call(
+        finish_body,
+        in_specs=[pl.BlockSpec(memory_space=pltpu.VMEM), pl.BlockSpec(memory_space=pltpu.VMEM)],
+        out_specs=pl.BlockSpec(memory_space=pltpu.HBM),
+        out_shape=pltpu.HBM(weights.shape, weights.dtype),
+        scratch_shapes=[pltpu.VMEM(weights.shape, weights.dtype), pltpu.SemaphoreType.DMA((STEPS,))],
+        compiler_params=limits,
+    )(pltpu.with_memory_space_constraint(weights, pltpu.VMEM), pltpu.with_memory_space_constraint(back, pltpu.VMEM))
 
 
 def local(gradients, momentum, weights):
     direction, new_momentum = direction_of(gradients, momentum)
     mats, rows, wide = direction.shape
-    sources = lax.axis_size(SHARD)
-    every = (*SHARD, "model")
-    x = lax.all_to_all(direction, every, 0, 0, tiled=True)
-    y, new_momentum = updated(x.reshape(sources, -1, rows, wide), new_momentum)
-    back = lax.all_to_all(y.reshape(mats, rows, wide), every, 0, 0, tiled=True)
-    return (weights - learn_rate * back, new_momentum)
+    sizes = tuple(lax.axis_size(axis) for axis in EVERY)
+    x = lax.all_to_all(direction, EVERY, 0, 0, tiled=True)
+    y, new_momentum = updated(x.reshape(*sizes, rows, wide), new_momentum)
+    back = lax.all_to_all(y.reshape(mats, rows, wide), EVERY, 0, 0, tiled=True)
+    return (finished(weights, back), new_momentum)
 
 
 def solution(mesh):
-    finer = Mesh(
-        mesh.devices.reshape(4, 4, 2, mesh.shape["model"]),
-        (*SHARD, "model"),
-    )
-    placed = P(None, SHARD, "model")
+    finer = Mesh(mesh.devices.reshape(4, 4, 2, 2, 4), (*SHARD, *MODEL))
+    placed = P(None, SHARD, MODEL)
     return jax.shard_map(
         local,
         mesh=finer,

time: 140 us -> 138 us (0.986)
  other arithmetic: 2.04 us -> 0 us
    sub x1 -> x0, other arithmetic: 2.04 us -> none  [local(): return (weights - learn_rate * back, new_momentum)]
    pallas_call x0 -> x1, Pallas kernels: none -> 1.41 us  [finished(): pl.pallas_call(finish_body, in_specs=[pl.BlockSpec(memory_space=pltpu.VME...]
where the time goes in v4:
time: 138 us
  blocking collectives  128 us (93%)
  Pallas kernels  8.46 us (6%)
    all_to_all x1, blocking collectives, local(): x = lax.all_to_all(direction, EVERY, 0, 0, tiled=True)  68.9 us
    all_to_all x1, blocking collectives, local(): back = lax.all_to_all(y.reshape(mats, rows, wide), EVERY, 0, 0, tiled=True)  59.6 us
    pallas_call x1, Pallas kernels, updated(): pl.pallas_call(update_body, in_specs=[pl.BlockSpec(memory_space=pltpu.VME...  4.71 us

profile of v4, /device:TPU:1, one launch (start us, length us, event | category | flops | bytes accessed | tf_op | source)
XLA Modules:
  0.0 137.6 jit_solution(16374535094704858733)
XLA Ops:
  0.6 2.3 %shard_map.50 = (f32[256,4,512]{2,1,0:T(4,128)S(1)}, f32[256,4,512]{2,1,0:T(4,128)S(1)}) custom-call(f32[256,4,512]{2,1,0:T(4,128)} %gradients_ref.1, f32[256,4,512]{2,1,0:T(4,128)} %momentum_ref.1), custom_call_target="tpu_custom_call" | custom-call | tf_op jit(solution)/shard_map/pallas_call | solution.py:46
  3.0 68.9 %all_to_all.10 = f32[256,4,512]{2,1,0:T(4,128)S(1)} all-to-all(f32[256,4,512]{2,1,0:T(4,128)S(1)} %get-tuple-element.6), channel_id=1, replica_groups=mesh['shard_0'=4,'shard_1'=4,'shard_2'=2,'model_0'=2,'model_1'=4] {'shar..., dimensions={0} | all-to-all | bytes 4194304 | tf_op jit(solution)/shard_map/all_to_all | solution.py:182
  71.9 4.7 %shard_map.51 = (f32[2,2,4,4,4,4,512]{6,5,4,3,2,1,0:T(4,128)S(1)}, f32[256,4,512]{2,1,0:T(4,128)}) custom-call(f32[2,2,4,4,4,4,512]{6,5,4,3,2,1,0:T(4,128)S(1)} %bitcast.2, f32[256,4,512]{2,1,0:T(4,128)S(1)} %get-tuple-element.7.momentum_ref), custom_call_target="tpu_custom_call" | custom-call | tf_op jit(solution)/shard_map/pallas_call | solution.py:142
  76.6 0.0 copy-start
  76.6 59.6 %all_to_all.11.back_ref = f32[256,4,512]{2,1,0:T(4,128)S(1)} all-to-all(f32[256,4,512]{2,1,0:T(4,128)S(1)} %bitcast.3), channel_id=1, replica_groups=mesh['shard_0'=4,'shard_1'=4,'shard_2'=2,'model_0'=2,'model_1'=4] {'shar..., dimensions={0} | all-to-all | bytes 4194304 | tf_op jit(solution)/shard_map/all_to_all | solution.py:184
  136.2 0.0 copy-done
  136.2 1.4 %shard_map.52 = f32[256,4,512]{2,1,0:T(4,128)} custom-call(f32[256,4,512]{2,1,0:T(4,128)S(1)} %copy-done, f32[256,4,512]{2,1,0:T(4,128)S(1)} %all_to_all.11.back_ref), custom_call_target="tpu_custom_call" | custom-call | tf_op jit(solution)/shard_map/pallas_call | solution.py:168
Async XLA Ops:
  76.6 59.6 %copy-start = (f32[256,4,512]{2,1,0:T(4,128)S(1)}, f32[256,4,512]{2,1,0:T(4,128)}, u32[]{:S(2)}) copy-start(f32[256,4,512]{2,1,0:T(4,128)} %weights_ref.1) | copy-start | bytes 6291460

commit v5 on v4

--- a/solution.py
+++ b/solution.py
@@ -9,7 +9,19 @@
 ITERS = 4
 SHARD = ("shard_0", "shard_1", "shard_2")
 MODEL = ("model_0", "model_1")
-EVERY = ("shard_2", "model_0", "shard_0", "shard_1", "model_1")
+EVERY = (*SHARD, *MODEL)
+ROWS = 32
+PARTS = 8
+
+
+def device_at(position):
+    ring, core, y, x = position // 32, position // 16 % 2, position // 4 % 4, position % 4
+    return ((ring % 4 * 4 + y) * 2 + core) * PARTS + ring // 4 * 4 + x
+
+
+ORDER = [device_at(-131 * i % (ROWS * PARTS)) for i in range(ROWS * PARTS)]
+PLACES = [[ORDER.index(row * PARTS + part) for row in range(ROWS)] for part in range(PARTS)]
+
 STEPS = 8
 
 hold_rate = 0.9
@@ -109,10 +121,10 @@
     keep.start()
     side = pieces_ref.shape[0] // 3
     wide = x_ref.shape[-1]
-    parts = [(i, j) for i in range(x_ref.shape[1]) for j in range(x_ref.shape[4])]
+    height = x_ref.shape[1]
     upper = lower = None
-    for k, (i, j) in enumerate(parts):
-        first, second, third = in_parts(x_ref[:, i, :, :, j].reshape(side, wide))
+    for k, places in enumerate(PLACES):
+        first, second, third = in_parts(jnp.concatenate([x_ref[i] for i in places], axis=0))
         pieces = jnp.concatenate([third, first, second], axis=0)
         pieces_ref[:, k * wide : (k + 1) * wide] = pieces
         half = pieces.shape[0] // 2
@@ -127,18 +139,18 @@
     small = (small + small.T) + sums[2 * side :, side:]
     small = small + (sums[2 * side :, :side] + sums[side : 2 * side, side:])
     left = on_left(polynomial(sums[side : 2 * side, :side] + small))
-    for k, (i, j) in enumerate(parts):
+    for k, places in enumerate(PLACES):
         columns = slice(k * wide, (k + 1) * wide)
         large = pieces_ref[side:, columns]
         right = jnp.concatenate([large, large, pieces_ref[: 2 * side, columns]], axis=0)
         new = jnp.dot(left, right, preferred_element_type=jnp.float32)
-        out_ref[:, i, :, :, j] = new.reshape(out_ref[:, i, :, :, j].shape)
+        for row, i in enumerate(places):
+            out_ref[i] = new[row * height : (row + 1) * height]
     keep.wait()
 
 
 def updated(x, momentum):
-    _, halves, _, _, blocks, _, wide = x.shape
-    columns = halves * blocks * wide
+    columns = PARTS * x.shape[-1]
     return pl.pallas_call(
         update_body,
         in_specs=[pl.BlockSpec(memory_space=pltpu.VMEM), pl.BlockSpec(memory_space=pltpu.VMEM)],
@@ -177,11 +189,9 @@
 
 def local(gradients, momentum, weights):
     direction, new_momentum = direction_of(gradients, momentum)
-    mats, rows, wide = direction.shape
-    sizes = tuple(lax.axis_size(axis) for axis in EVERY)
-    x = lax.all_to_all(direction, EVERY, 0, 0, tiled=True)
-    y, new_momentum = updated(x.reshape(*sizes, rows, wide), new_momentum)
-    back = lax.all_to_all(y.reshape(mats, rows, wide), EVERY, 0, 0, tiled=True)
+    x = lax.all_to_all(direction, EVERY, 0, 0, tiled=True, axis_index_groups=[ORDER])
+    y, new_momentum = updated(x, new_momentum)
+    back = lax.all_to_all(y, EVERY, 0, 0, tiled=True, axis_index_groups=[ORDER])
     return (finished(weights, back), new_momentum)
 
 

time: 138 us -> 137 us (level)
  no operation moved by 1% of the time
where the time goes in v5:
time: 137 us
  blocking collectives  128 us (93%)
  Pallas kernels  8.46 us (6%)
    all_to_all x1, blocking collectives, local(): lax.all_to_all(direction, EVERY, 0, 0, tiled=True, axis_index_groups=[ORD...  68.5 us
    all_to_all x1, blocking collectives, local(): back = lax.all_to_all(y, EVERY, 0, 0, tiled=True, axis_index_groups=[ORDER])  59.3 us
    pallas_call x1, Pallas kernels, updated(): pl.pallas_call(update_body, in_specs=[pl.BlockSpec(memory_space=pltpu.VME...  4.72 us

profile of v5, /device:TPU:1, one launch (start us, length us, event | category | flops | bytes accessed | tf_op | source)
XLA Modules:
  0.0 136.9 jit_solution(12611507718963022607)
XLA Ops:
  0.6 2.3 %shard_map.50 = (f32[256,4,512]{2,1,0:T(4,128)S(1)}, f32[256,4,512]{2,1,0:T(4,128)S(1)}) custom-call(f32[256,4,512]{2,1,0:T(4,128)} %gradients_ref.1, f32[256,4,512]{2,1,0:T(4,128)} %momentum_ref.1), custom_call_target="tpu_custom_call" | custom-call | tf_op jit(solution)/shard_map/pallas_call | solution.py:58
  3.0 68.5 %all_to_all.10.x_ref = f32[256,4,512]{2,1,0:T(4,128)S(1)} all-to-all(f32[256,4,512]{2,1,0:T(4,128)S(1)} %get-tuple-element.6), channel_id=1, replica_groups={{0,249,238,219,220,201,246,227,228,209,198,187,188,169,158,139,140,177,..., dimensions={0} | all-to-all | bytes 4194304 | tf_op jit(solution)/shard_map/all_to_all | solution.py:192
  71.5 4.7 %shard_map.51 = (f32[256,4,512]{2,1,0:T(4,128)S(1)}, f32[256,4,512]{2,1,0:T(4,128)}) custom-call(f32[256,4,512]{2,1,0:T(4,128)S(1)} %all_to_all.10.x_ref, f32[256,4,512]{2,1,0:T(4,128)S(1)} %get-tuple-element.7.momentum_ref), custom_call_target="tpu_custom_call" | custom-call | tf_op jit(solution)/shard_map/pallas_call | solution.py:154
  76.2 0.0 copy-start
  76.2 59.3 %all_to_all.11.back_ref = f32[256,4,512]{2,1,0:T(4,128)S(1)} all-to-all(f32[256,4,512]{2,1,0:T(4,128)S(1)} %get-tuple-element.8), channel_id=1, replica_groups={{0,249,238,219,220,201,246,227,228,209,198,187,188,169,158,139,140,177,..., dimensions={0} | all-to-all | bytes 4194304 | tf_op jit(solution)/shard_map/all_to_all | solution.py:194
  135.5 0.0 copy-done
  135.5 1.4 %shard_map.52 = f32[256,4,512]{2,1,0:T(4,128)} custom-call(f32[256,4,512]{2,1,0:T(4,128)S(1)} %copy-done, f32[256,4,512]{2,1,0:T(4,128)S(1)} %all_to_all.11.back_ref), custom_call_target="tpu_custom_call" | custom-call | tf_op jit(solution)/shard_map/pallas_call | solution.py:180
Async XLA Ops:
  76.2 59.4 %copy-start = (f32[256,4,512]{2,1,0:T(4,128)S(1)}, f32[256,4,512]{2,1,0:T(4,128)}, u32[]{:S(2)}) copy-start(f32[256,4,512]{2,1,0:T(4,128)} %weights_ref.1) | copy-start | bytes 6291460
